TPU v7x, 128 devices: a whole 4x4x4 slice. The times are simulated.
128 devices in a mesh: freq: 8 (over x, z_hi), panel: 16 (over z_lo, y, core).
Axes of the slice: x: 4, y: 4, z: 4 (z_hi: 2, z_lo: 2; z = z_hi * 2 + z_lo), core: 2. Of those that a mesh axis runs over, the one named last changes fastest.
Arguments:
- traces: bfloat16 [640, 640, 1024], P('panel', 'freq'), may hold values from -6 to 6
- filters: float32 [16, 7, 64], replicated, may hold values from -0.25 to 0.25
Outputs:
- primaries: bfloat16 [640, 640, 1024], P('panel', 'freq')
All inputs are finite; a program needn't handle non-finite values.
Results may differ from a plain program's by a relative error of at most 0.0095.
Values may be sent and summed in bfloat16 or wider, within the bound.
No kernel may reach another device: no remote copies, remote signals or barrier semaphores. Data moves between devices by JAX's collectives and lax.ppermute only.
A program may use at most 128 MiB of HBM per device.

v0:
```python
import math
import jax
import jax.numpy as jnp
from jax import lax
from jax.sharding import PartitionSpec as P

NS = 640
NT = 1024
NF = 96
FLO = 8
TAPS = 64
SPAN = 7
RWIN = 40


def wave_table(freq_bins, sample_index):
    phases = freq_bins[:, None] * sample_index[None, :] % NT
    angles = phases.astype(jnp.float32) * jnp.float32(2.0 * math.pi / NT)
    return (jnp.cos(angles), jnp.sin(angles))


def complex_product(left_side, right_side):

    def factor_product(leading_factor, trailing_factor):
        return jnp.einsum(
            "gjo,god->gjd", leading_factor, trailing_factor, preferred_element_type=jnp.float32
        )

    part_real = factor_product(left_side[0], right_side[0]) - factor_product(
        left_side[1], right_side[1]
    )
    part_imag = factor_product(left_side[0], right_side[1]) + factor_product(
        left_side[1], right_side[0]
    )
    return jnp.stack([part_real, part_imag])


def response(filters, freq_bins):
    tap_index = jnp.arange(TAPS, dtype=jnp.int32)
    cosine_wave, sine_wave = wave_table(freq_bins, tap_index)
    filter_real = jnp.einsum("fk,wjk->fjw", cosine_wave, filters)
    filter_imag = -jnp.einsum("fk,wjk->fjw", sine_wave, filters)
    return (jnp.repeat(filter_real, RWIN, axis=2), jnp.repeat(filter_imag, RWIN, axis=2))


def apply_filter(extended, filter_real, filter_imag, source_count):
    sum_real = jnp.zeros(extended.shape[1:2] + (source_count,) + extended.shape[3:], jnp.float32)
    sum_imag = jnp.zeros_like(sum_real)
    for shifted in range(SPAN):
        part_real = extended[0, :, shifted : shifted + source_count, :]
        part_imag = extended[1, :, shifted : shifted + source_count, :]
        weight_real = filter_real[:, shifted][:, None, :]
        weight_imaginary = filter_imag[:, shifted][:, None, :]
        sum_real = sum_real + weight_real * part_real - weight_imaginary * part_imag
        sum_imag = sum_imag + weight_real * part_imag + weight_imaginary * part_real
    return jnp.stack([sum_real, sum_imag])


def per_device(traces, filters):
    shot_rows, receiver_cols, time_sample_count = traces.shape
    rim_width = SPAN // 2
    scale_sources = jnp.float32(math.sqrt(NS))
    freq_bins = FLO + jnp.arange(NF, dtype=jnp.int32)
    cosine_wave, sine_wave = wave_table(freq_bins, jnp.arange(NT, dtype=jnp.int32))
    forward = (jnp.concatenate([cosine_wave, -sine_wave], 0) / jnp.float32(math.sqrt(NT))).astype(
        jnp.bfloat16
    )
    reciprocal_value = jnp.concatenate([cosine_wave, -sine_wave], 0).astype(jnp.bfloat16)
    spectra = jnp.einsum("srt,ct->csr", traces, forward, preferred_element_type=jnp.float32)
    spectra = spectra.astype(jnp.bfloat16).reshape(2, NF, shot_rows, receiver_cols)
    columns = lax.all_to_all(spectra, "panel", split_axis=1, concat_axis=2, tiled=True)
    slice_count = columns.shape[1]
    first_slice = lax.axis_index("panel") * slice_count
    complete = lax.all_gather(columns, "freq", axis=3, tiled=True)
    order_one = (complex_product(complete, columns) / scale_sources).astype(jnp.bfloat16)
    order_two = complex_product(complete, order_one) / scale_sources
    prediction = (order_one.astype(jnp.float32) - order_two).astype(jnp.bfloat16)
    extended = jnp.pad(
        prediction.astype(jnp.float32), ((0, 0), (0, 0), (rim_width, rim_width), (0, 0))
    )
    own_bins = FLO + first_slice + jnp.arange(slice_count, dtype=jnp.int32)
    filter_real, filter_imag = response(filters, own_bins)
    receiver_start = lax.axis_index("freq") * receiver_cols
    filter_real = lax.dynamic_slice_in_dim(filter_real, receiver_start, receiver_cols, 2)
    filter_imag = lax.dynamic_slice_in_dim(filter_imag, receiver_start, receiver_cols, 2)
    matched = apply_filter(extended, filter_real, filter_imag, NS)
    returned = lax.all_to_all(
        matched.astype(jnp.bfloat16), "panel", split_axis=2, concat_axis=1, tiled=True
    )
    matched_rows = returned.reshape(2 * NF, shot_rows, receiver_cols)
    multiples = jnp.einsum(
        "csr,ct->srt", matched_rows, reciprocal_value, preferred_element_type=jnp.float32
    )
    multiples = multiples / jnp.float32(math.sqrt(NF))
    return (traces.astype(jnp.float32) - multiples).astype(jnp.bfloat16)


def solution(mesh):
    placed = (P("panel", "freq", None), P())
    return jax.shard_map(
        per_device, mesh=mesh, in_specs=placed, out_specs=P("panel", "freq", None), check_vma=False
    )
```

profile of v0, /device:TPU:1, one launch (start us, length us, event | category | flops | bytes accessed | tf_op | source)
XLA Modules:
  0.0 312.2 jit_solution(14349941599640643925)
XLA Ops:
  6.5 1.6 fusion.58
  8.2 0.8 copy-done.4
  8.9 0.2 copy-done.6
  9.1 4.8 %convolution_convert_fusion = bf16[192,40,80]{0,2,1:T(8,128)(2,1)S(1)} fusion(bf16[40,80,1024]{2,1,0:T(8,128)(2,1)} %param.2, f32[96,1024]{1,0:T(8,128)S(1)} %get-tuple-element.24, f32[96,1024]{1,0:T(8,128)S(1)} %get-tuple-element.23), kind=kOutput, calls=%fused_computation.35 | convolution fusion | flops 1259495424 | bytes 8568832 | tf_op jit(solution)/shard_map/srt,ct->csr/dot_general | solution.py:69
  13.9 0.9 reshape.26
  14.7 3.3 %copy.54 = bf16[2,96,40,80]{3,2,0,1:T(8,128)(2,1)} copy(bf16[2,96,40,80]{1,0,3,2:T(2,128)(2,1)S(1)} %reshape.26) | data formatting | bytes 2457600 | tf_op jit(solution)/shard_map/reshape | solution.py:70
  18.1 32.3 %all_to_all.33 = bf16[2,96,40,80]{3,2,0,1:T(8,128)(2,1)S(1)} all-to-all(bf16[2,96,40,80]{3,2,0,1:T(8,128)(2,1)} %copy.54), channel_id=1, replica_groups=mesh['freq'=8,'panel'=16] {'panel'}, dimensions={1} | all-to-all | bytes 2457600 | tf_op jit(solution)/shard_map/all_to_all | solution.py:71
  50.4 1.7 copy.56
  52.2 4.5 %copy.57 = bf16[2,6,640,80]{2,0,1,3:T(2,128)(2,1)} copy(bf16[2,6,640,80]{3,2,1,0:T(8,128)(2,1)} %bitcast.140) | data formatting | bytes 2457600 | tf_op jit(solution)/shard_map/all_to_all | solution.py:71
  56.7 0.0 all-gather.2.cloned.1.call-update
  56.8 0.2 convolution_bitcast_fusion
  57.0 0.2 broadcast_in_dim.4
  57.2 0.2 reshape.25
  57.4 0.2 fusion.45
  57.7 0.2 broadcast_in_dim.5
  57.8 0.2 reshape.27
  58.1 0.2 constant_dynamic-slice_fusion.10
  58.4 0.3 copy.55
  58.7 0.3 fusion.81
  59.1 0.1 copy.62
  59.2 0.1 copy.59
  59.3 118.6 %all-gather.2.cloned.1.call-done = bf16[2,6,640,640]{2,0,1,3:T(2,128)(2,1)} async-done(((bf16[2,6,640,80]{2,0,1,3:T(2,128)(2,1)}), bf16[2,6,640,640]{2,0,1,3:T(2,128)(2,1)}) %all-gather.2.cloned.1.call-update) | async-done | bytes 9830416 | tf_op jit(solution)/shard_map/all_gather | solution.py:74
  177.9 20.6 %fusion.80 = (bf16[1,6,640,640]{2,0,1,3:T(2,128)(2,1)}, bf16[1,6,640,640]{2,0,1,3:T(2,128)(2,1)}) fusion(bf16[2,6,640,640]{2,0,1,3:T(2,128)(2,1)} %all-gather.2.cloned.1.call-done), kind=kLoop, calls=%fused_computation.122 | loop fusion | bytes 19660800 | tf_op jit(solution)/shard_map/slice | solution.py:29
  198.5 19.7 %copy.91 = bf16[1,6,640,640]{3,2,1,0:T(8,128)(2,1)} copy(bf16[1,6,640,640]{2,0,1,3:T(2,128)(2,1)} %get-tuple-element.6) | data formatting | bytes 9830400
  218.3 19.8 %copy.90 = bf16[1,6,640,640]{3,2,1,0:T(8,128)(2,1)} copy(bf16[1,6,640,640]{2,0,1,3:T(2,128)(2,1)} %get-tuple-element.5) | data formatting | bytes 9830400
  238.0 4.2 %fusion.6 = f32[6,640,80]{1,2,0:T(8,128)S(1)} fusion(bf16[6,640,80]{2,1,0:T(8,128)(2,1)S(1)} %bitcast.133, bf16[1,6,640,640]{3,2,1,0:T(8,128)(2,1)} %copy.91), kind=kOutput, calls=%fused_computation.7 | convolution fusion | flops 393216000 | bytes 6758400 | tf_op jit(solution)/shard_map/gjo,god->gjd/dot_general | solution.py:25
  242.2 1.7 fusion.4
  243.9 0.7 copy-done.3
  244.6 1.7 fusion.23
  246.3 1.7 fusion.29
  247.9 0.2 fusion.16
  248.2 1.7 fusion.2
  249.8 1.7 fusion
  251.5 1.7 fusion.35
  253.2 1.7 fusion.41
  254.8 0.4 fusion.44
  255.2 5.4 %subtract_convert_fusion.1 = bf16[1,6,640,80]{2,3,1,0:T(8,128)(2,1)S(1)} fusion(f32[2,6,640,80]{2,3,1,0:T(8,128)S(1)} %fusion.44, f32[6,80]{1,0:T(8,128)S(1)} %bitcast.143, f32[6,80]{1,0:T(8,128)S(1)} %bitcast.145, f32[6,80]{1,0:T(8,128)S(1)} %bitcast.147, f32[6,80]{1,0:T(8,128)S(1)} %bitcast.149, f32[6,80]{1,0:T(8,128)S(1)} %bitcast.151, ...), kind=kLoop, calls=%fused_computation.47 | loop fusion | flops 8601600 | bytes 5586944 | tf_op jit(solution)/shard_map/convert
  260.6 5.3 %add_convert_fusion = bf16[1,6,640,80]{2,3,1,0:T(8,128)(2,1)S(1)} fusion(f32[2,6,640,80]{2,3,1,0:T(8,128)S(1)} %fusion.44, f32[6,80]{1,0:T(8,128)S(1)} %bitcast.144, f32[6,80]{1,0:T(8,128)S(1)} %bitcast.146, f32[6,80]{1,0:T(8,128)S(1)} %bitcast.148, f32[6,80]{1,0:T(8,128)S(1)} %bitcast.150, f32[6,80]{1,0:T(8,128)S(1)} %bitcast.152, ...), kind=kLoop, calls=%fused_computation.46 | loop fusion | flops 8601600 | bytes 5586944 | tf_op jit(solution)/shard_map/convert.1
  265.9 0.1 pad_maximum_fusion
  266.1 2.6 copy.67
  268.6 0.0 slice-start
  268.7 30.9 %all_to_all.34 = bf16[2,6,640,80]{3,0,1,2:T(2,128)(2,1)S(1)} all-to-all(bf16[2,6,640,80]{3,0,1,2:T(2,128)(2,1)S(1)} %copy.67), channel_id=1, replica_groups=mesh['freq'=8,'panel'=16] {'panel'}, dimensions={2} | all-to-all | bytes 2457600 | tf_op jit(solution)/shard_map/all_to_all | solution.py:87
  299.5 0.4 copy.68
  299.9 0.3 copy.69
  300.3 0.9 slice-done.1
  301.2 0.1 copy-done.5
  301.3 0.1 copy-done.7
  301.4 4.0 %subtract_convert_fusion = bf16[40,80,1024]{2,1,0:T(8,128)(2,1)} fusion(bf16[40,80,1024]{2,1,0:T(8,128)(2,1)S(1)} %bitcast.142, bf16[192,40,80]{2,1,0:T(8,128)(2,1)S(1)} %bitcast.138, f32[96,1024]{1,0:T(8,128)S(1)} %copy-done.7, f32[96,1024]{1,0:T(8,128)S(1)} %copy-done.5), kind=kOutput, calls=%fused_computation | convolution fusion | flops 1272184832 | bytes 15122432 | tf_op jit(solution)/shard_map/csr,ct->srt/dot_general | solution.py:91
  (33 shorter events, 0.1 us)
Async XLA Ops:
  6.5 50.2 %copy-start = (f32[16,7,64]{2,0,1:T(8,128)S(1)}, f32[16,7,64]{2,0,1:T(8,128)}, u32[]{:S(2)}) copy-start(f32[16,7,64]{2,0,1:T(8,128)} %param.3) | copy-start | bytes 86020
  6.5 171.3 %all-gather.2.cloned.1.call-start = ((), (), s32[]{:S(2)}) async-start(), calls=%async_computation.2 | async-start | bytes 11059200 | tf_op jit(solution)/shard_map/all_gather | solution.py:74
  8.2 0.8 copy-start.4
  8.2 0.9 copy-start.6
  238.0 4.2 %copy-start.2 = (bf16[1,6,640,640]{3,2,1,0:T(8,128)(2,1)S(1)}, bf16[1,6,640,640]{3,2,1,0:T(8,128)(2,1)}, u32[]{:S(2)}) copy-start(bf16[1,6,640,640]{3,2,1,0:T(8,128)(2,1)} %copy.91) | copy-start | bytes 14745604
  242.2 2.4 copy-start.3
  268.6 31.6 %slice-start = ((s8[6553600]{0:T(1024)(128)(4,1)}), s8[4194304]{0:T(1024)(128)(4,1)S(1)}, s32[]{:S(2)}) async-start(s8[6553600]{0:T(1024)(128)(4,1)} %bitcast.141), calls=%async_computation.3 | async-start | bytes 8388608
  299.5 1.7 slice-start.1
  299.9 1.4 copy-start.5
  299.9 1.5 copy-start.7
  301.4 4.0 %copy-start.1 = (f32[16,7,64]{2,0,1:T(8,128)S(1)}, f32[16,7,64]{2,0,1:T(8,128)}, u32[]{:S(2)}) copy-start(f32[16,7,64]{2,0,1:T(8,128)} %param.3) | copy-start | bytes 86020
Sparse Core Ops, SparseCore 0:
  56.8 120.9 all-gather.1
where the time goes:
time: 314 us; the launch traced here: 312 us
  waiting for transfers between devices  119 us (38%)
  local copies, waits for them, and re-layouts  78.6 us (25%)
  blocking collectives  63.2 us (20%)
  matrix products  25 us (8%)
  between operations  13.7 us (4%)
  other arithmetic  13.1 us (4%)
    all_gather x1, waiting for transfers between devices, per_device(): complete = lax.all_gather(columns, 'freq', axis=3, tiled=True)  119 us
    unnamed x36, local copies, waits for them, and re-layouts  42.4 us
    all_to_all x1, blocking collectives, per_device(): lax.all_to_all(spectra, 'panel', split_axis=1, concat_axis=2, tiled=True)  32.3 us
    all_to_all x1, blocking collectives, per_device(): lax.all_to_all(matched.astype(jnp.bfloat16), 'panel', split_axis=2, conca...  30.9 us
    slice x1, local copies, waits for them, and re-layouts, complex_product(): left_side[0]  20.6 us
    dot_general x8, matrix products, factor_product(): jnp.einsum('gjo,god->gjd', leading_factor, trailing_factor, preferred_ele...  15.8 us
    another operation x2, other arithmetic  10.7 us
    all_to_all x3, local copies, waits for them, and re-layouts, per_device(): lax.all_to_all(spectra, 'panel', split_axis=1, concat_axis=2, tiled=True)  6.6 us
  transfers between devices with their start and end apart: 1, of which 1 were waited for; matrix products, arithmetic and copies ran while one was open for 1% of the time, Pallas kernels for 0%

commit v1 on v0

--- a/solution.py
+++ b/solution.py
@@ -71,7 +71,8 @@
     columns = lax.all_to_all(spectra, "panel", split_axis=1, concat_axis=2, tiled=True)
     slice_count = columns.shape[1]
     first_slice = lax.axis_index("panel") * slice_count
-    complete = lax.all_gather(columns, "freq", axis=3, tiled=True)
+    blocks = lax.all_gather(columns, "freq")
+    complete = jnp.concatenate(blocks, axis=3)
     order_one = (complex_product(complete, columns) / scale_sources).astype(jnp.bfloat16)
     order_two = complex_product(complete, order_one) / scale_sources
     prediction = (order_one.astype(jnp.float32) - order_two).astype(jnp.bfloat16)

time: 314 us -> 262 us (0.83)
  local copies, waits for them, and re-layouts: 78.6 us -> 32.8 us
  matrix products: 25 us -> 19.6 us
    unnamed x36 -> x32, local copies, waits for them, and re-layouts: 42.4 us -> 2.4 us
    slice x1, local copies, waits for them, and re-layouts: 20.6 us -> 6.98 us  [complex_product(): left_side[1]]
    all_gather x0 -> x2, local copies, waits for them, and re-layouts: none -> 12.4 us  [per_device(): blocks = lax.all_gather(columns, 'freq')]
    dot_general x8, matrix products: 15.8 us -> 10.4 us  [factor_product(): jnp.einsum('gjo,god->gjd', leading_factor, trailing_factor, preferred_ele...]
    all_to_all x3 -> x2, local copies, waits for them, and re-layouts: 6.6 us -> 2.07 us  [per_device(): lax.all_to_all(spectra, 'panel', split_axis=1, concat_axis=2, tiled=True)]
where the time goes in v1:
time: 262 us; the launch traced here: 261 us
  waiting for transfers between devices  119 us (45%)
  blocking collectives  63.2 us (24%)
  local copies, waits for them, and re-layouts  32.8 us (13%)
  matrix products  19.6 us (7%)
  between operations  13.8 us (5%)
  other arithmetic  13.3 us (5%)
    all_gather x1, waiting for transfers between devices, per_device(): blocks = lax.all_gather(columns, 'freq')  119 us
    all_to_all x1, blocking collectives, per_device(): lax.all_to_all(spectra, 'panel', split_axis=1, concat_axis=2, tiled=True)  32.3 us
    all_to_all x1, blocking collectives, per_device(): lax.all_to_all(matched.astype(jnp.bfloat16), 'panel', split_axis=2, conca...  30.9 us
    all_gather x2, local copies, waits for them, and re-layouts, per_device(): blocks = lax.all_gather(columns, 'freq')  12.4 us
    another operation x2, other arithmetic  10.9 us
    dot_general x8, matrix products, factor_product(): jnp.einsum('gjo,god->gjd', leading_factor, trailing_factor, preferred_ele...  10.4 us
    slice x1, local copies, waits for them, and re-layouts, complex_product(): left_side[1]  6.98 us
  transfers between devices with their start and end apart: 1, of which 1 were waited for; matrix products, arithmetic and copies ran while one was open for 1% of the time, Pallas kernels for 0%

profile of v1, /device:TPU:1, one launch (start us, length us, event | category | flops | bytes accessed | tf_op | source)
XLA Modules:
  0.0 261.3 jit_solution(4636179896849813843)
XLA Ops:
  6.5 0.0 copy-start
  6.5 1.6 fusion.24
  8.2 0.7 copy-done.3
  8.9 0.1 copy-done.5
  9.0 4.8 %convolution_convert_fusion = bf16[192,40,80]{0,2,1:T(8,128)(2,1)S(1)} fusion(bf16[40,80,1024]{2,1,0:T(8,128)(2,1)} %param.2, f32[96,1024]{1,0:T(8,128)S(1)} %get-tuple-element.24, f32[96,1024]{1,0:T(8,128)S(1)} %get-tuple-element.23), kind=kOutput, calls=%fused_computation.20 | convolution fusion | flops 1259495424 | bytes 8568832 | tf_op jit(solution)/shard_map/srt,ct->csr/dot_general | solution.py:69
  13.8 0.9 reshape.35
  14.7 3.3 %copy.55 = bf16[2,96,40,80]{3,2,0,1:T(8,128)(2,1)} copy(bf16[2,96,40,80]{1,0,3,2:T(2,128)(2,1)S(1)} %reshape.35) | data formatting | bytes 2457600 | tf_op jit(solution)/shard_map/reshape | solution.py:70
  18.0 32.3 %all_to_all.30 = bf16[2,96,40,80]{3,2,0,1:T(8,128)(2,1)S(1)} all-to-all(bf16[2,96,40,80]{3,2,0,1:T(8,128)(2,1)} %copy.55), channel_id=1, replica_groups=mesh['freq'=8,'panel'=16] {'panel'}, dimensions={1} | all-to-all | bytes 2457600 | tf_op jit(solution)/shard_map/all_to_all | solution.py:71
  50.4 1.7 copy.57
  52.1 3.7 %copy.58 = bf16[1,2,6,640,80]{3,4,2,1,0:T(8,128)(2,1)} copy(bf16[1,2,6,640,80]{4,3,2,1,0:T(8,128)(2,1)} %bitcast.128) | data formatting | bytes 2457600 | tf_op jit(solution)/shard_map/all_gather | solution.py:74
  55.8 0.0 all-gather.2.cloned.1.call-update
  55.9 0.2 convolution_bitcast_fusion
  56.1 0.2 broadcast_in_dim.4
  56.3 0.2 reshape.34
  56.5 0.2 fusion.9
  56.8 0.2 broadcast_in_dim.5
  57.0 0.2 reshape.37
  57.2 0.2 constant_dynamic-slice_fusion.10
  57.5 0.3 copy.56
  57.9 0.3 fusion.47
  58.2 0.1 copy.60
  58.3 0.1 copy.63
  58.4 118.6 %all-gather.2.cloned.1.call-done = bf16[8,2,6,640,80]{3,4,2,1,0:T(8,128)(2,1)} async-done(((bf16[1,2,6,640,80]{3,4,2,1,0:T(8,128)(2,1)}), bf16[8,2,6,640,80]{3,4,2,1,0:T(8,128)(2,1)}) %all-gather.2.cloned.1.call-update) | async-done | bytes 9830416 | tf_op jit(solution)/shard_map/all_gather | solution.py:74
  177.0 8.7 %copy.123 = bf16[8,2,6,640,80]{3,4,0,2,1:T(8,128)(2,1)} copy(bf16[8,2,6,640,80]{3,4,2,1,0:T(8,128)(2,1)} %all-gather.2.cloned.1.call-done) | data formatting | bytes 19660800 | tf_op jit(solution)/shard_map/all_gather | solution.py:74
  185.7 7.0 %fusion.46 = (bf16[1,6,640,8,80]{2,4,3,1,0:T(8,128)(2,1)S(1)}, bf16[1,6,640,8,80]{2,4,3,1,0:T(8,128)(2,1)}) fusion(bf16[2,6,640,8,80]{2,4,3,1,0:T(8,128)(2,1)} %bitcast.119), kind=kLoop, calls=%fused_computation.109 | loop fusion | bytes 19660800 | tf_op jit(solution)/shard_map/slice | solution.py:30
  192.7 3.5 %fusion.50 = f32[6,640,80]{1,2,0:T(8,128)S(1)} fusion(bf16[6,640,640]{1,2,0:T(8,128)(2,1)} %bitcast.115, bf16[6,640,80]{2,1,0:T(8,128)(2,1)S(1)} %bitcast.121), kind=kOutput, calls=%fused_computation.113 | convolution fusion | flops 393216000 | bytes 6758400 | tf_op jit(solution)/shard_map/gjo,god->gjd/dot_general | solution.py:25
  196.2 0.3 copy-done.2
  196.6 1.0 fusion.51
  197.5 1.0 fusion.4
  198.5 1.0 fusion.5
  199.5 0.2 fusion
  199.8 1.0 fusion.11
  200.8 1.0 fusion.12
  201.8 1.0 fusion.6
  202.7 1.0 fusion.7
  203.7 0.4 fusion.8
  204.1 5.6 %subtract_convert_fusion.1 = bf16[1,6,640,80]{2,3,1,0:T(8,128)(2,1)S(1)} fusion(f32[2,6,640,80]{2,3,1,0:T(8,128)S(1)} %fusion.8, f32[6,80]{1,0:T(8,128)S(1)} %bitcast.153, f32[6,80]{1,0:T(8,128)S(1)} %bitcast.155, f32[6,80]{1,0:T(8,128)S(1)} %bitcast.157, f32[6,80]{1,0:T(8,128)S(1)} %bitcast.131, f32[6,80]{1,0:T(8,128)S(1)} %bitcast.133, ...), kind=kLoop, calls=%fused_computation.32 | loop fusion | flops 8601600 | bytes 5586944 | tf_op jit(solution)/shard_map/convert
  209.7 5.3 %add_convert_fusion = bf16[1,6,640,80]{2,3,1,0:T(8,128)(2,1)S(1)} fusion(f32[2,6,640,80]{2,3,1,0:T(8,128)S(1)} %fusion.8, f32[6,80]{1,0:T(8,128)S(1)} %bitcast.154, f32[6,80]{1,0:T(8,128)S(1)} %bitcast.156, f32[6,80]{1,0:T(8,128)S(1)} %bitcast.158, f32[6,80]{1,0:T(8,128)S(1)} %bitcast.132, f32[6,80]{1,0:T(8,128)S(1)} %bitcast.134, f32[6,80]{1,0:T(8,128)S(1)} %bitcast.136, ...), kind=kLoop, calls=%fused_computation.31 | loop fusion | flops 8601600 | bytes 5586944 | tf_op jit(solution)/shard_map/convert.1
  215.0 0.1 pad_maximum_fusion
  215.2 2.6 copy.75
  217.7 0.0 slice-start
  217.7 30.9 %all_to_all.31 = bf16[2,6,640,80]{3,0,1,2:T(2,128)(2,1)S(1)} all-to-all(bf16[2,6,640,80]{3,0,1,2:T(2,128)(2,1)S(1)} %copy.75), channel_id=1, replica_groups=mesh['freq'=8,'panel'=16] {'panel'}, dimensions={2} | all-to-all | bytes 2457600 | tf_op jit(solution)/shard_map/all_to_all | solution.py:88
  248.6 0.4 copy.76
  249.0 0.3 copy.77
  249.3 0.9 slice-done.1
  250.3 0.1 copy-done.4
  250.4 0.1 copy-done.6
  250.5 4.0 %subtract_convert_fusion = bf16[40,80,1024]{2,1,0:T(8,128)(2,1)} fusion(bf16[40,80,1024]{2,1,0:T(8,128)(2,1)S(1)} %bitcast.130, bf16[192,40,80]{2,1,0:T(8,128)(2,1)S(1)} %bitcast.126, f32[96,1024]{1,0:T(8,128)S(1)} %copy-done.6, f32[96,1024]{1,0:T(8,128)S(1)} %copy-done.4), kind=kOutput, calls=%fused_computation | convolution fusion | flops 1272184832 | bytes 15122432 | tf_op jit(solution)/shard_map/csr,ct->srt/dot_general | solution.py:92
  (30 shorter events, 0.1 us)
Async XLA Ops:
  6.5 49.3 %copy-start = (f32[16,7,64]{2,0,1:T(8,128)S(1)}, f32[16,7,64]{2,0,1:T(8,128)}, u32[]{:S(2)}) copy-start(f32[16,7,64]{2,0,1:T(8,128)} %param.3) | copy-start | bytes 86020
  6.5 170.5 %all-gather.2.cloned.1.call-start = ((), (), s32[]{:S(2)}) async-start(), calls=%async_computation.2 | async-start | bytes 11059200 | tf_op jit(solution)/shard_map/all_gather | solution.py:74
  8.2 0.7 copy-start.3
  8.2 0.9 copy-start.5
  192.7 3.9 %copy-start.2 = (bf16[1,6,640,8,80]{2,4,3,1,0:T(8,128)(2,1)S(1)}, bf16[1,6,640,8,80]{2,4,3,1,0:T(8,128)(2,1)}, u32[]{:S(2)}) copy-start(bf16[1,6,640,8,80]{2,4,3,1,0:T(8,128)(2,1)} %get-tuple-element.6) | copy-start | bytes 14745604
  217.7 31.6 %slice-start = ((s8[6553600]{0:T(1024)(128)(4,1)}), s8[4194304]{0:T(1024)(128)(4,1)S(1)}, s32[]{:S(2)}) async-start(s8[6553600]{0:T(1024)(128)(4,1)} %bitcast.129), calls=%async_computation.3 | async-start | bytes 8388608
  248.6 1.7 slice-start.1
  249.0 1.4 copy-start.4
  249.0 1.5 copy-start.6
  250.5 4.0 %copy-start.1 = (f32[16,7,64]{2,0,1:T(8,128)S(1)}, f32[16,7,64]{2,0,1:T(8,128)}, u32[]{:S(2)}) copy-start(f32[16,7,64]{2,0,1:T(8,128)} %param.3) | copy-start | bytes 86020
Sparse Core Ops, SparseCore 0:
  56.0 121.0 all-gather.1
